TPU v7x, 256 devices: a whole 4x4x8 slice. The times are simulated.
256 devices in a mesh: rows: 128 (over z, y, x_lo, core), grp: 2 (over x_hi).
Axes of the slice: x: 4 (x_hi: 2, x_lo: 2; x = x_hi * 2 + x_lo), y: 4, z: 8, core: 2. Of those that a mesh axis runs over, the one named last changes fastest.
Arguments:
- region_id: int32 [1048576], P(('rows', 'grp')), may hold values from 0 to 63
- product_id: int32 [1048576], P(('rows', 'grp')), may hold values from 0 to 63
- measures: bfloat16 [1048576, 256], P(('rows', 'grp')), may hold values from -1 to 1
- slot_of_cell: int32 [4096], replicated, may hold values from 0 to 4095, each once
Outputs:
- cube: float32 [4096, 256], P(('rows', 'grp'))
- region_totals: float32 [64, 256], replicated
- product_totals: float32 [64, 256], replicated
All inputs are finite; a program needn't handle non-finite values.
Results may differ from a plain program's by a relative error of at most 0.0003.
Values sent between devices are 32-bit elements; how exact they have to be, the bound alone decides.
No kernel may reach another device: no remote copies, remote signals or barrier semaphores. Data moves between devices by JAX's collectives and lax.ppermute only.
A program may use at most 64 MiB of HBM per device.

v0:
```python
import math

import jax
import jax.numpy as jnp
from jax import lax
from jax.sharding import Mesh
from jax.sharding import PartitionSpec as P

REGIONS = 64
PRODUCTS = 64
ROWS = ("rows_0", "rows_1", "rows_2", "rows_3")
ROWS_GRP = ("rows_0", "rows_1", "rows_2", "rows_3", "grp")


def cut_along(array, dim, devices):
    before, after = (array.shape[:dim], array.shape[dim + 1 :])
    return jnp.moveaxis(array.reshape(*before, devices, -1, *after), dim, 0)


def sent_and_summed(array, axis, dim):
    devices = lax.axis_size(axis)
    pieces = lax.all_to_all(cut_along(array, dim, devices), axis, 0, 0, tiled=True)
    return jnp.sum(pieces, axis=0)


def sum_in_two_steps(array, axes, dim):
    far, near = axes
    pieces = cut_along(array, dim, lax.axis_size(far))
    nearer = sent_and_summed(pieces, near, dim + 1)
    arrived = lax.all_to_all(nearer, far, split_axis=0, concat_axis=0, tiled=True)
    return arrived.sum(axis=0)


def block_sums(slot, measures, start, count):
    width = math.gcd(count, 512)

    def one_block(first):
        labels = first + lax.iota(jnp.int32, width)
        onehot = (slot[None, :] == labels[:, None]).astype(measures.dtype)
        return jnp.dot(onehot, measures, preferred_element_type=jnp.float32)

    firsts = start + jnp.arange(count // width, dtype=jnp.int32) * width
    sums = lax.map(one_block, firsts)
    return sums.reshape(count, measures.shape[1])


def label_totals_out(labels, count, weights):
    onehot = (labels[None, :] == lax.iota(jnp.int32, count)[:, None]).astype(weights.dtype)
    return jnp.dot(
        onehot, weights, precision=lax.Precision.HIGHEST, preferred_element_type=jnp.float32
    )


def on_device(region_id, product_id, measures, slot_of_cell):
    cells = slot_of_cell.shape[0]
    width = measures.shape[1]
    n_rows = lax.axis_size(ROWS)
    n_grp = lax.axis_size("grp")
    owned_count = cells // (n_rows * n_grp)
    cell = region_id * PRODUCTS + product_id
    slot = jnp.take(slot_of_cell, cell)
    partial_value = block_sums(slot, measures, 0, cells).reshape(n_rows, n_grp, owned_count, width)
    partial_value = sum_in_two_steps(partial_value, (("rows_0", "rows_1", "rows_2"), "rows_3"), 0)
    partial_value = sent_and_summed(partial_value, "grp", 1)
    cube = partial_value.reshape(owned_count, width)
    region_portion = label_totals_out(region_id, REGIONS, measures)
    product_part = label_totals_out(product_id, PRODUCTS, measures)
    region_totals, product_totals = lax.psum((region_portion, product_part), ROWS_GRP)
    return (cube, region_totals, product_totals)


def solution(mesh):
    split = Mesh(
        mesh.devices.reshape(8, 4, 2, 2, mesh.shape["grp"]),
        ("rows_0", "rows_1", "rows_2", "rows_3", "grp"),
    )
    in_specs = (P(ROWS_GRP), P(ROWS_GRP), P(ROWS_GRP, None), P())
    out_specs = (P(ROWS_GRP, None), P(), P())
    return jax.shard_map(
        on_device, mesh=split, in_specs=in_specs, out_specs=out_specs, check_vma=False
    )
```

profile of v0, /device:TPU:1, one launch (start us, length us, event | category | flops | bytes accessed | tf_op | source)
XLA Modules:
  0.0 352.5 jit_solution(768593017855653590)
XLA Ops:
  7.2 0.0 copy-start
  7.2 0.7 broadcast_clamp_fusion
  7.9 0.0 copy-done
  8.0 0.0 copy-start.2
  8.0 0.0 copy-start.3
  8.0 0.0 copy-start.1
  8.0 23.0 %gather_fusion = s32[4096]{0:T(1024)S(1)} fusion(s32[4096]{0:T(1024)S(1)} %copy-done, s32[4096]{0:T(1024)S(1)} %broadcast_clamp_fusion), kind=kCustom, calls=%fused_computation | custom fusion | bytes 49152 | tf_op jit(solution)/shard_map/jit(_take)/gather | solution.py:61
  31.0 0.0 copy-done.2
  31.1 26.8 %while.10 = (s32[]{:T(128)}, f32[8,512,256]{2,1,0:T(8,128)}, s32[4096]{0:T(1024)S(1)}, s32[8]{0:T(128)S(1)}, bf16[4096,256]{1,0:T(8,128)(2,1)S(1)}, /*index=5*/s32[]{:T(128)}) while((s32[]{:T(128)}, f32[8,512,256]{2,1,0:T(8,128)}, s32[4096]{0:T(1024)S(1)}, s32[8]{0:T(128)S(1)}, bf16[4096,256]{1,0:T(8,128)(2,1)S(1)}, /*index=5*/s32[]{:T(128)}) %tuple.29), condition=%wide.region_1.2_spmd, body=%wide.region_0.1_spmd.sunk | while | flops 1075839488 | bytes 2642017 | solution.py:43
  31.1 0.6 dynamic_slice.5
  31.7 0.6 iota_add_fusion.2
  32.3 2.1 fusion.22
  34.4 0.6 dynamic_slice.5
  35.0 0.6 iota_add_fusion.2
  35.7 2.1 fusion.22
  37.8 0.6 dynamic_slice.5
  38.4 0.6 iota_add_fusion.2
  39.0 2.1 fusion.22
  41.1 0.6 dynamic_slice.5
  41.7 0.6 iota_add_fusion.2
  42.4 2.1 fusion.22
  44.5 0.6 dynamic_slice.5
  45.1 0.6 iota_add_fusion.2
  45.7 2.1 fusion.22
  47.8 0.6 dynamic_slice.5
  48.4 0.6 iota_add_fusion.2
  49.1 2.1 fusion.22
  51.2 0.6 dynamic_slice.5
  51.8 0.6 iota_add_fusion.2
  52.4 2.1 fusion.22
  54.5 0.6 dynamic_slice.5
  55.1 0.6 iota_add_fusion.2
  55.8 2.1 fusion.22
  57.9 2.6 copy.7
  60.5 11.0 %all_to_all.15 = f32[2,64,1,2,16,256]{5,4,3,1,2,0:T(8,128)} all-to-all(f32[2,64,1,2,16,256]{5,4,3,1,2,0:T(8,128)S(1)} %copy.7), channel_id=1, replica_groups=mesh['rows_0'=8,'rows_1'=4,'rows_2'=2,'rows_3'=2,'grp'=2] {'rows_3'}, dimensions={0} | all-to-all | bytes 8388608 | tf_op jit(solution)/shard_map/all_to_all | solution.py:22
  71.5 4.2 %reduce_sum.29 = f32[64,2,16,256]{3,2,1,0:T(8,128)} reduce(f32[2,64,1,2,16,256]{5,4,3,1,2,0:T(8,128)} %all_to_all.15, f32[]{:T(128)} %constant.17.clone.1), dimensions={0,2}, to_apply=%region_2.3 | reduce | flops 524288 | bytes 6291460 | tf_op jit(solution)/shard_map/reduce_sum | solution.py:23
  75.7 11.3 %all-to-all-start.1 = ((f32[64,1,2,16,256]{4,3,2,1,0:T(8,128)}), f32[64,1,2,16,256]{4,3,2,1,0:T(8,128)}, u32[]{:S(2)}, u32[]{:S(2)}) async-start(f32[64,1,2,16,256]{4,3,2,1,0:T(8,128)} %bitcast.4), calls=%async_computation.1 | async-start | bytes 4194304 | tf_op jit(solution)/shard_map/all_to_all | solution.py:30
  87.0 0.0 all-reduce.3.cloned.1.call-start
  87.1 1.0 fusion.10
  88.1 1.0 fusion.11
  89.2 0.0 all-reduce.3.cloned.1.call-update
  89.2 46.5 %all-to-all-done.1 = f32[64,1,2,16,256]{4,3,2,1,0:T(8,128)} async-done(((f32[64,1,2,16,256]{4,3,2,1,0:T(8,128)}), f32[64,1,2,16,256]{4,3,2,1,0:T(8,128)}, u32[]{:S(2)}, u32[]{:S(2)}) %all-to-all-start.1) | async-done | bytes 2097184 | tf_op jit(solution)/shard_map/all_to_all | solution.py:30
  135.7 1.7 reduce_sum.31
  137.4 7.8 %all_to_all.16 = f32[2,1,1,16,256]{4,3,2,1,0:T(8,128)S(1)} all-to-all(f32[2,1,1,16,256]{4,3,2,1,0:T(8,128)S(1)} %bitcast.20), channel_id=1, replica_groups=mesh['rows_0'=8,'rows_1'=4,'rows_2'=2,'rows_3'=2,'grp'=2] {'grp'}, dimensions={0} | all-to-all | bytes 65536 | tf_op jit(solution)/shard_map/all_to_all | solution.py:22
  145.3 0.6 reduce_sum.32
  145.9 196.9 %all-reduce.3.cloned.1.call-done = (f32[64,256]{1,0:T(8,128)}, f32[64,256]{1,0:T(8,128)}) async-done(((f32[64,256]{1,0:T(8,128)}, f32[64,256]{1,0:T(8,128)}), (f32[64,256]{1,0:T(8,128)}, f32[64,256]{1,0:T(8,128)})) %all-reduce.3.cloned.1.call-update) | async-done | bytes 131088 | tf_op jit(solution)/shard_map/psum | solution.py:68
  342.7 1.5 copy.19
  344.2 1.5 copy.20
  (5 shorter events, 0.0 us)
Async XLA Ops:
  7.2 0.8 copy-start
  8.0 23.1 %copy-start.2 = (s32[4096]{0:T(1024)S(1)}, s32[4096]{0:T(1024)}, u32[]{:S(2)}) copy-start(s32[4096]{0:T(1024)} %param.6) | copy-start | bytes 49156
  8.0 23.1 %copy-start.3 = (s32[4096]{0:T(1024)S(1)}, s32[4096]{0:T(1024)}, u32[]{:S(2)}) copy-start(s32[4096]{0:T(1024)} %param.7) | copy-start | bytes 49156
  8.0 23.1 %copy-start.1 = (bf16[4096,256]{1,0:T(8,128)(2,1)S(1)}, bf16[4096,256]{1,0:T(8,128)(2,1)}, u32[]{:S(2)}) copy-start(bf16[4096,256]{1,0:T(8,128)(2,1)} %param.8) | copy-start | bytes 6291460
  75.7 60.0 %all-to-all-start.1 = ((f32[64,1,2,16,256]{4,3,2,1,0:T(8,128)}), f32[64,1,2,16,256]{4,3,2,1,0:T(8,128)}, u32[]{:S(2)}, u32[]{:S(2)}) async-start(f32[64,1,2,16,256]{4,3,2,1,0:T(8,128)} %bitcast.4), calls=%async_computation.1 | async-start | bytes 4194304 | tf_op jit(solution)/shard_map/all_to_all | solution.py:30
  87.0 255.7 %all-reduce.3.cloned.1.call-start = ((), (), s32[]{:S(2)}) async-start(), calls=%async_computation.3 | async-start | bytes 262144 | tf_op jit(solution)/shard_map/psum | solution.py:68
Sparse Core Ops, SparseCore 0:
  94.0 248.6 all-reduce.2
where the time goes:
time: 353 us
  waiting for transfers between devices  243 us (69%)
  local copies, waits for them, and re-layouts  33.3 us (9%)
  matrix products  19 us (5%)
  blocking collectives  18.8 us (5%)
  between operations  14.1 us (4%)
  other arithmetic  12.5 us (4%)
  starting transfers between devices  11.4 us (3%)
    psum x1, waiting for transfers between devices, on_device(): lax.psum((region_portion, product_part), ROWS_GRP)  197 us
    all_to_all x1, waiting for transfers between devices, sum_in_two_steps(): lax.all_to_all(nearer, far, split_axis=0, concat_axis=0, tiled=True)  46.5 us
    gather x1, local copies, waits for them, and re-layouts, on_device(): slot = jnp.take(slot_of_cell, cell)  23 us
    all_to_all x2, blocking collectives, sent_and_summed(): lax.all_to_all(cut_along(array, dim, devices), axis, 0, 0, tiled=True)  18.8 us
    dot_general x8, matrix products, one_block(): return jnp.dot(onehot, measures, preferred_element_type=jnp.float32)  16.9 us
    all_to_all x1, starting transfers between devices, sum_in_two_steps(): lax.all_to_all(nearer, far, split_axis=0, concat_axis=0, tiled=True)  11.3 us
  transfers between devices with their start and end apart: 2, of which 2 were waited for; matrix products, arithmetic and copies ran while one was open for 1% of the time, Pallas kernels for 0%

commit v1 on v0

v1 whole, which is shorter than its diff:
```python
import functools

import jax
import jax.numpy as jnp
from jax import lax
from jax.experimental import pallas as pl
from jax.experimental.pallas import tpu as pltpu
from jax.sharding import Mesh
from jax.sharding import PartitionSpec as P

Z, Y, XL, CORE, XH = "rows_0", "rows_1", "rows_2", "rows_3", "grp"
ALL = (Z, Y, XL, CORE, XH)
PLANE = (Y, XL, XH)
PLANE_CORES = (Y, XL, CORE, XH)
WIDTH = 256
SIDE = 64
BF16, F32 = jnp.bfloat16, jnp.float32
VMEM = pl.BlockSpec(memory_space=pltpu.VMEM)
SMEM = pl.BlockSpec(memory_space=pltpu.SMEM)


def prep_body(core_ref, region_ref, product_ref, table_ref, group_ref, line_ref):
    table = table_ref[...]
    high, low = table >> 6, table & 63
    line = (high >> 3) * 8 + (low & 7)
    plane = (high & 7) * 2 + ((low >> 4) & 1)
    group = ((low >> 3) & 1) * 32 + ((low >> 5) ^ core_ref[0]) * 16 + plane
    both = jnp.concatenate([group, line], axis=1).astype(F32).astype(BF16)
    label = lax.broadcasted_iota(jnp.int32, (SIDE, region_ref.shape[1]), 0)
    in_region = (label == region_ref[...]).astype(F32).astype(BF16)
    found = lax.dot_general(both, in_region, (((0,), (0,)), ((), ())), preferred_element_type=F32)
    in_product = label == product_ref[...]
    for half, out in ((found[:SIDE], group_ref), (found[SIDE:], line_ref)):
        out[...] = jnp.sum(jnp.where(in_product, half, 0.0), axis=0, keepdims=True).astype(jnp.int32)


def prep(core, region, product, table):
    row = jax.ShapeDtypeStruct(region.shape, jnp.int32)
    return pl.pallas_call(
        prep_body,
        out_shape=[row, row],
        in_specs=[SMEM, VMEM, VMEM, VMEM],
        out_specs=[VMEM, VMEM],
        cost_estimate=pl.CostEstimate(flops=2 * 10**9, bytes_accessed=10**5, transcendentals=0),
        name="prep",
    )(core, region, product, table)


def block_body(first, per_dot, with_totals, adds, *refs):
    refs = list(refs)
    group_ref, line_ref, measures_ref = refs[:3]
    del refs[:3]
    label_ref = refs.pop(0) if with_totals else None
    other_ref = refs.pop(0) if adds else None
    out_ref, one_line, lhs = refs
    n = group_ref.shape[1]
    label = lax.broadcasted_iota(jnp.int32, (SIDE, n), 0)
    one_line[...] = (label == line_ref[...]).astype(F32).astype(BF16)

    def step(b, _):
        for k in range(per_dot):
            chosen = (group_ref[...] == first + b * per_dot + k).astype(F32).astype(BF16)
            lhs[k * SIDE : (k + 1) * SIDE, :] = one_line[...] * chosen
        sums = jnp.dot(lhs[...], measures_ref[...], preferred_element_type=F32)
        for k in range(per_dot):
            piece = sums[k * SIDE : (k + 1) * SIDE]
            if adds:
                piece = piece + other_ref[b * per_dot + k, 0:SIDE, :]
            out_ref[b * per_dot + k, 0:SIDE, :] = piece
        return 0

    lax.fori_loop(0, 16 // per_dot, step, 0)
    if with_totals:
        member = (label == label_ref[...]).astype(F32).astype(BF16)
        totals = jnp.dot(member, measures_ref[...], preferred_element_type=F32)
        for g in range(16):
            piece = totals[4 * g : 4 * g + 4]
            if adds:
                piece = piece + other_ref[g, SIDE : SIDE + 4, :]
            out_ref[g, SIDE : SIDE + 4, :] = piece
            out_ref[g, SIDE + 4 : SIDE + 8, :] = jnp.zeros((4, WIDTH), F32)


def block(first, group, line, measures, label=None, other=None):
    per_dot = 8
    n = group.shape[1]
    height = SIDE if label is None else SIDE + 8
    args = [group, line, measures] + [a for a in (label, other) if a is not None]
    return pl.pallas_call(
        functools.partial(block_body, first, per_dot, label is not None, other is not None),
        out_shape=jax.ShapeDtypeStruct((16, height, WIDTH), F32),
        in_specs=[VMEM] * len(args),
        out_specs=VMEM,
        scratch_shapes=[pltpu.VMEM((SIDE, n), BF16), pltpu.VMEM((SIDE * per_dot, n), BF16)],
        compiler_params=pltpu.CompilerParams(vmem_limit_bytes=24 << 20),
        cost_estimate=pl.CostEstimate(
            flops=2 * 1024 * n * WIDTH, bytes_accessed=3 << 20, transcendentals=0
        ),
        name="block",
    )(*args)


def to_partner(array):
    return lax.ppermute(array, CORE, [(0, 1), (1, 0)])


def exchange(array, axes):
    return lax.all_to_all(array, axes, 0, 0, tiled=True)


def on_device(region_id, product_id, measures, slot_of_cell):
    core = lax.axis_index(CORE)
    region, product = region_id[None, :], product_id[None, :]
    group, line = prep(core[None], region, product, slot_of_cell.reshape(SIDE, SIDE))
    kept_label = jnp.where(core == 0, region, product)
    sent_label = jnp.where(core == 0, product, region)
    after = lax.optimization_barrier

    sent_a = block(16, group, line, measures, label=sent_label)
    got_a = to_partner(sent_a)
    group, sent_a = after((group, sent_a))
    sent_b = block(48, group, line, measures)
    got_b = to_partner(sent_b)
    group, sent_b, got_a = after((group, sent_b, got_a))
    chip_a = block(0, group, line, measures, label=kept_label, other=got_a)
    near_a = exchange(chip_a, PLANE)
    group, chip_a, got_b = after((group, chip_a, got_b))
    chip_b = block(32, group, line, measures, other=got_b)
    near_b = exchange(chip_b, PLANE)

    column_a = jnp.sum(near_a, axis=0)
    totals = jnp.broadcast_to(column_a[SIDE:][None], (8, 8, WIDTH))
    far_a = exchange(jnp.concatenate([column_a[:SIDE].reshape(8, 8, WIDTH), totals], axis=1), Z)
    column_b = jnp.sum(near_b, axis=0)
    far_b = exchange(column_b.reshape(8, 8, WIDTH), Z)
    cube_a = jnp.sum(far_a, axis=0)
    spread = exchange(jnp.broadcast_to(cube_a[None, 8:12], (32, 4, WIDTH)), PLANE_CORES)
    cube = jnp.concatenate([cube_a[:8], jnp.sum(far_b, axis=0)], axis=0)
    spread = spread.reshape(8, 2, 2, 4, WIDTH).swapaxes(0, 1).reshape(2, SIDE, WIDTH)
    return cube, spread[0], spread[1]


def solution(mesh):
    split = Mesh(mesh.devices.reshape(8, 4, 2, 2, mesh.shape["grp"]), ALL)
    in_specs = (P(ALL), P(ALL), P(ALL, None), P())
    out_specs = (P(ALL, None), P(), P())
    return jax.shard_map(
        on_device, mesh=split, in_specs=in_specs, out_specs=out_specs, check_vma=False
    )
```

time: 353 us -> 109 us (0.31)
  waiting for transfers between devices: 243 us -> 45.7 us
  local copies, waits for them, and re-layouts: 33.3 us -> 4.85 us
  starting transfers between devices: 11.4 us -> 35.7 us
  matrix products: 19 us -> 0 us
  blocking collectives: 18.8 us -> 0 us
  Pallas kernels: 0 us -> 16.5 us
  between operations: 14.1 us -> 0.77 us
  other arithmetic: 12.5 us -> 4.07 us
    psum x1 -> x0, waiting for transfers between devices: 197 us -> none  [on_device(): lax.psum((region_portion, product_part), ROWS_GRP)]
    gather x1 -> x0, local copies, waits for them, and re-layouts: 23 us -> none  [on_device(): slot = jnp.take(slot_of_cell, cell)]
    all_to_all x1 -> x5, starting transfers between devices: 11.3 us -> 32.4 us  [exchange(): return lax.all_to_all(array, axes, 0, 0, tiled=True)]
    dot_general x10 -> x0, matrix products: 19 us -> none  [the longest x8 16.9 us: one_block(): return jnp.dot(onehot, measures, preferred_element_type=jnp.float32)]
    all_to_all x2 -> x0, blocking collectives: 18.8 us -> none  [sent_and_summed(): lax.all_to_all(cut_along(array, dim, devices), axis, 0, 0, tiled=True)]
    pallas_call x0 -> x5, Pallas kernels: none -> 16.5 us  [the longest x4 14.3 us: block(): pl.pallas_call(functools.partial(block_body, first, per_dot, label is not...]
    add x8 -> x0, other arithmetic: 5.17 us -> none  [one_block(): labels = first + lax.iota(jnp.int32, width)]
    dynamic_slice x8 -> x0, local copies, waits for them, and re-layouts: 4.66 us -> none  [block_sums(): sums = lax.map(one_block, firsts)]
  transfers between devices with their start and end apart: 2 -> 7, of which waited for: 2 -> 5; matrix products, arithmetic and copies ran while one was open for 1% -> 3% of each run, Pallas kernels for 0% -> 10%
where the time goes in v1:
time: 109 us; the launch traced here: 108 us
  waiting for transfers between devices  45.7 us (42%)
  starting transfers between devices  35.7 us (33%)
  Pallas kernels  16.5 us (15%)
  local copies, waits for them, and re-layouts  4.85 us (4%)
  other arithmetic  4.07 us (4%)
    all_to_all x5, waiting for transfers between devices, exchange(): return lax.all_to_all(array, axes, 0, 0, tiled=True)  45.7 us
    all_to_all x5, starting transfers between devices, exchange(): return lax.all_to_all(array, axes, 0, 0, tiled=True)  32.4 us
    pallas_call x4, Pallas kernels, block(): pl.pallas_call(functools.partial(block_body, first, per_dot, label is not...  14.3 us
    ppermute x2, starting transfers between devices, to_partner(): return lax.ppermute(array, CORE, [(0, 1), (1, 0)])  3.31 us
    pallas_call x1, Pallas kernels, prep(): pl.pallas_call(prep_body, out_shape=[row, row], in_specs=[SMEM, VMEM, VME...  2.2 us
  transfers between devices with their start and end apart: 7, of which 5 were waited for; matrix products, arithmetic and copies ran while one was open for 3% of the time, Pallas kernels for 10%

profile of v1, /device:TPU:1, one launch (start us, length us, event | category | flops | bytes accessed | tf_op | source)
XLA Modules:
  0.0 107.6 jit_solution(17079070177073784734)
XLA Ops:
  0.6 1.4 %reshape.27.table_ref = s32[64,64]{1,0:T(8,128)} reshape(s32[4096]{0:T(1024)} %param.7) | data formatting | bytes 32768 | tf_op jit(solution)/shard_map/reshape | solution.py:114
  2.0 0.7 broadcast_select_fusion
  2.8 0.0 copy-start
  2.8 2.2 %prep.1 = (s32[1,4096]{1,0:T(1,128)}, s32[1,4096]{1,0:T(1,128)}) custom-call(s32[1]{0:T(128)} %bitcast.core_ref, s32[1,4096]{1,0:T(1,128)} %bitcast.18, s32[1,4096]{1,0:T(1,128)} %bitcast.19, s32[64,64]{1,0:T(8,128)} %reshape.27.table_ref), custom_call_target="tpu_custom_call" | custom-call | flops 2000000000 | bytes 100000 | tf_op jit(solution)/shard_map/prep/pallas_call | solution.py:39
  5.0 0.0 copy-done
  5.0 0.0 copy-start.1
  5.0 0.7 copy-done.1
  5.7 0.0 copy-start.3
  5.7 0.7 copy-done.3
  6.4 3.1 %block.4 = f32[16,72,256]{2,1,0:T(8,128)S(1)} custom-call(s32[1,4096]{1,0:T(1,128)S(1)} %copy-done.1, s32[1,4096]{1,0:T(1,128)S(1)} %copy-done.3, bf16[4096,256]{1,0:T(8,128)(2,1)S(1)} %copy-done, s32[1,4096]{1,0:T(1,128)S(1)} %bitcast.16), custom_call_target="tpu_custom_call" | custom-call | flops 2147483648 | bytes 3145728 | tf_op jit(solution)/shard_map/block/pallas_call | solution.py:89
  9.5 3.3 %collective-permute-start = (f32[16,72,256]{2,1,0:T(8,128)S(1)}, f32[16,72,256]{2,1,0:T(8,128)S(1)}, u32[]{:S(2)}, u32[]{:S(2)}) collective-permute-start(f32[16,72,256]{2,1,0:T(8,128)S(1)} %block.4), channel_id=1, source_target_pairs={{0,2},{2,0},{1,3},{3,1},{4,6},{6,4},{5,7},{7,5},{8,10},{10,8},{9,1... | collective-permute-start | bytes 3538952 | tf_op jit(solution)/shard_map/ppermute | solution.py:104
  12.8 3.6 %block.5 = f32[16,64,256]{2,1,0:T(8,128)} custom-call(s32[1,4096]{1,0:T(1,128)S(1)} %copy-done.1, s32[1,4096]{1,0:T(1,128)S(1)} %copy-done.3, bf16[4096,256]{1,0:T(8,128)(2,1)S(1)} %copy-done), custom_call_target="tpu_custom_call" | custom-call | flops 2147483648 | bytes 3145728 | tf_op jit(solution)/shard_map/block/pallas_call | solution.py:89
  16.4 0.0 collective-permute-start.1
  16.4 0.0 collective-permute-done.refs_4_
  16.4 4.1 %block.6 = f32[16,72,256]{2,1,0:T(8,128)} custom-call(s32[1,4096]{1,0:T(1,128)S(1)} %copy-done.1, s32[1,4096]{1,0:T(1,128)S(1)} %copy-done.3, bf16[4096,256]{1,0:T(8,128)(2,1)S(1)} %copy-done, s32[1,4096]{1,0:T(1,128)S(1)} %bitcast.15, f32[16,72,256]{2,1,0:T(8,128)S(1)} %collective-permute-done.refs_4_), custom_call_target="tpu_custom_call" | custom-call | flops 2147483648 | bytes 3145728 | tf_op jit(solution)/shard_map/block/pallas_call | solution.py:89
  20.5 0.0 copy-start.2
  20.5 0.0 copy-start.4
  20.5 5.2 %all-to-all-start = ((f32[16,72,256]{2,1,0:T(8,128)}), f32[16,72,256]{2,1,0:T(8,128)}, u32[]{:S(2)}, u32[]{:S(2)}) async-start(f32[16,72,256]{2,1,0:T(8,128)} %block.6), calls=%async_computation | async-start | bytes 2359296 | tf_op jit(solution)/shard_map/all_to_all | solution.py:108
  25.7 0.0 collective-permute-done.1.refs_3_
  25.7 0.0 copy-done.2
  25.8 0.0 copy-done.4
  25.8 3.6 %block.7 = f32[16,64,256]{2,1,0:T(8,128)} custom-call(s32[1,4096]{1,0:T(1,128)S(1)} %copy-done.2, s32[1,4096]{1,0:T(1,128)S(1)} %copy-done.4, bf16[4096,256]{1,0:T(8,128)(2,1)S(1)} %copy-done, f32[16,64,256]{2,1,0:T(8,128)S(1)} %collective-permute-done.1.refs_3_), custom_call_target="tpu_custom_call" | custom-call | flops 2147483648 | bytes 3145728 | tf_op jit(solution)/shard_map/block/pallas_call | solution.py:89
  29.4 12.9 %all-to-all-done = f32[16,72,256]{2,1,0:T(8,128)} async-done(((f32[16,72,256]{2,1,0:T(8,128)}), f32[16,72,256]{2,1,0:T(8,128)}, u32[]{:S(2)}, u32[]{:S(2)}) %all-to-all-start) | async-done | bytes 1179680 | tf_op jit(solution)/shard_map/all_to_all | solution.py:108
  42.3 5.1 %all-to-all-start.2 = ((f32[16,64,256]{2,1,0:T(8,128)}), f32[16,64,256]{2,1,0:T(8,128)S(1)}, u32[]{:S(2)}, u32[]{:S(2)}) async-start(f32[16,64,256]{2,1,0:T(8,128)} %block.7), calls=%async_computation.2 | async-start | bytes 2097152 | tf_op jit(solution)/shard_map/all_to_all | solution.py:108
  47.4 1.3 %reduce_sum.36 = f32[72,256]{1,0:T(8,128)S(1)} reduce(f32[16,72,256]{2,1,0:T(8,128)} %all-to-all-done, f32[]{:T(128)} %constant.7.clone.1), dimensions={0}, to_apply=%region_0.1 | reduce | flops 276480 | bytes 1253380 | tf_op jit(solution)/shard_map/reduce_sum | solution.py:131
  48.8 0.7 pad_maximum_fusion
  49.4 11.6 %all-to-all-done.2 = f32[16,64,256]{2,1,0:T(8,128)S(1)} async-done(((f32[16,64,256]{2,1,0:T(8,128)}), f32[16,64,256]{2,1,0:T(8,128)S(1)}, u32[]{:S(2)}, u32[]{:S(2)}) %all-to-all-start.2) | async-done | bytes 1048608 | tf_op jit(solution)/shard_map/all_to_all | solution.py:108
  61.0 8.2 %all-to-all-start.1 = ((f32[8,16,256]{2,1,0:T(8,128)}), f32[8,16,256]{2,1,0:T(8,128)S(1)}, u32[]{:S(2)}, u32[]{:S(2)}) async-start(f32[8,16,256]{2,1,0:T(8,128)} %pad_maximum_fusion), calls=%async_computation.1 | async-start | bytes 262144 | tf_op jit(solution)/shard_map/all_to_all | solution.py:108
  69.2 0.7 reduce_sum.38
  69.9 7.2 %all-to-all-done.1 = f32[8,16,256]{2,1,0:T(8,128)S(1)} async-done(((f32[8,16,256]{2,1,0:T(8,128)}), f32[8,16,256]{2,1,0:T(8,128)S(1)}, u32[]{:S(2)}, u32[]{:S(2)}) %all-to-all-start.1) | async-done | bytes 131104 | tf_op jit(solution)/shard_map/all_to_all | solution.py:108
  77.1 3.4 %all-to-all-start.3 = ((f32[8,8,256]{2,1,0:T(8,128)}), f32[8,8,256]{2,1,0:T(8,128)S(1)}, u32[]{:S(2)}, u32[]{:S(2)}) async-start(f32[8,8,256]{2,1,0:T(8,128)} %bitcast.6), calls=%async_computation.3 | async-start | bytes 131072 | tf_op jit(solution)/shard_map/all_to_all | solution.py:108
  80.5 7.1 %all-to-all-done.3 = f32[8,8,256]{2,1,0:T(8,128)S(1)} async-done(((f32[8,8,256]{2,1,0:T(8,128)}), f32[8,8,256]{2,1,0:T(8,128)S(1)}, u32[]{:S(2)}, u32[]{:S(2)}) %all-to-all-start.3) | async-done | bytes 65568 | tf_op jit(solution)/shard_map/all_to_all | solution.py:108
  87.7 0.7 broadcast_in_dim.25
  88.3 10.5 %all-to-all-start.4 = ((f32[32,4,256]{2,1,0:T(4,128)}), f32[32,4,256]{2,1,0:T(4,128)S(1)}, u32[]{:S(2)}, u32[]{:S(2)}) async-start(f32[32,4,256]{2,1,0:T(4,128)} %broadcast_in_dim.25), calls=%async_computation.4 | async-start | bytes 262144 | tf_op jit(solution)/shard_map/all_to_all | solution.py:108
  98.9 0.6 pad_maximum_fusion.1
  99.5 6.8 %all-to-all-done.4 = f32[32,4,256]{2,1,0:T(4,128)S(1)} async-done(((f32[32,4,256]{2,1,0:T(4,128)}), f32[32,4,256]{2,1,0:T(4,128)S(1)}, u32[]{:S(2)}, u32[]{:S(2)}) %all-to-all-start.4) | async-done | bytes 131104 | tf_op jit(solution)/shard_map/all_to_all | solution.py:108
  106.3 0.7 squeeze.6
  106.9 0.7 squeeze.7
  (8 shorter events, 0.1 us)
Async XLA Ops:
  2.8 2.2 %copy-start = (bf16[4096,256]{1,0:T(8,128)(2,1)S(1)}, bf16[4096,256]{1,0:T(8,128)(2,1)}, u32[]{:S(2)}) copy-start(bf16[4096,256]{1,0:T(8,128)(2,1)} %refs_2_.7) | copy-start | bytes 6291460
  5.0 0.7 copy-start.1
  5.7 0.7 copy-start.3
  9.5 6.9 %collective-permute-start = (f32[16,72,256]{2,1,0:T(8,128)S(1)}, f32[16,72,256]{2,1,0:T(8,128)S(1)}, u32[]{:S(2)}, u32[]{:S(2)}) collective-permute-start(f32[16,72,256]{2,1,0:T(8,128)S(1)} %block.4), channel_id=1, source_target_pairs={{0,2},{2,0},{1,3},{3,1},{4,6},{6,4},{5,7},{7,5},{8,10},{10,8},{9,1... | collective-permute-start | bytes 3538952 | tf_op jit(solution)/shard_map/ppermute | solution.py:104
  16.4 9.4 %collective-permute-start.1 = (f32[16,64,256]{2,1,0:T(8,128)}, f32[16,64,256]{2,1,0:T(8,128)S(1)}, u32[]{:S(2)}, u32[]{:S(2)}) collective-permute-start(f32[16,64,256]{2,1,0:T(8,128)} %block.5), channel_id=1, source_target_pairs={{0,2},{2,0},{1,3},{3,1},{4,6},{6,4},{5,7},{7,5},{8,10},{10,8},{9,1... | collective-permute-start | bytes 3145736 | tf_op jit(solution)/shard_map/ppermute | solution.py:104
  20.5 5.3 %copy-start.2 = (s32[1,4096]{1,0:T(1,128)S(1)}, s32[1,4096]{1,0:T(1,128)}, u32[]{:S(2)}) copy-start(s32[1,4096]{1,0:T(1,128)} %get-tuple-element.15.refs_0_) | copy-start | bytes 49156
  20.5 5.3 %copy-start.4 = (s32[1,4096]{1,0:T(1,128)S(1)}, s32[1,4096]{1,0:T(1,128)}, u32[]{:S(2)}) copy-start(s32[1,4096]{1,0:T(1,128)} %get-tuple-element.11.refs_1_) | copy-start | bytes 49156
  20.5 21.8 %all-to-all-start = ((f32[16,72,256]{2,1,0:T(8,128)}), f32[16,72,256]{2,1,0:T(8,128)}, u32[]{:S(2)}, u32[]{:S(2)}) async-start(f32[16,72,256]{2,1,0:T(8,128)} %block.6), calls=%async_computation | async-start | bytes 2359296 | tf_op jit(solution)/shard_map/all_to_all | solution.py:108
  42.3 18.8 %all-to-all-start.2 = ((f32[16,64,256]{2,1,0:T(8,128)}), f32[16,64,256]{2,1,0:T(8,128)S(1)}, u32[]{:S(2)}, u32[]{:S(2)}) async-start(f32[16,64,256]{2,1,0:T(8,128)} %block.7), calls=%async_computation.2 | async-start | bytes 2097152 | tf_op jit(solution)/shard_map/all_to_all | solution.py:108
  61.0 16.1 %all-to-all-start.1 = ((f32[8,16,256]{2,1,0:T(8,128)}), f32[8,16,256]{2,1,0:T(8,128)S(1)}, u32[]{:S(2)}, u32[]{:S(2)}) async-start(f32[8,16,256]{2,1,0:T(8,128)} %pad_maximum_fusion), calls=%async_computation.1 | async-start | bytes 262144 | tf_op jit(solution)/shard_map/all_to_all | solution.py:108
  77.1 10.5 %all-to-all-start.3 = ((f32[8,8,256]{2,1,0:T(8,128)}), f32[8,8,256]{2,1,0:T(8,128)S(1)}, u32[]{:S(2)}, u32[]{:S(2)}) async-start(f32[8,8,256]{2,1,0:T(8,128)} %bitcast.6), calls=%async_computation.3 | async-start | bytes 131072 | tf_op jit(solution)/shard_map/all_to_all | solution.py:108
  88.3 17.9 %all-to-all-start.4 = ((f32[32,4,256]{2,1,0:T(4,128)}), f32[32,4,256]{2,1,0:T(4,128)S(1)}, u32[]{:S(2)}, u32[]{:S(2)}) async-start(f32[32,4,256]{2,1,0:T(4,128)} %broadcast_in_dim.25), calls=%async_computation.4 | async-start | bytes 262144 | tf_op jit(solution)/shard_map/all_to_all | solution.py:108

commit v2 on v0

v2 whole, which is shorter than its diff:
```python
import functools

import jax
import jax.numpy as jnp
from jax import lax
from jax.experimental import pallas as pl
from jax.experimental.pallas import tpu as pltpu
from jax.sharding import Mesh
from jax.sharding import PartitionSpec as P


Z, Y, XL, CORE, XH = "rows_0", "rows_1", "rows_2", "rows_3", "grp"
ALL = (Z, Y, XL, CORE, XH)
PLANE = (Y, XL, XH)
WIDTH = 256
SIDE = 64
PEERS = 16
LAYERS = 8
OWN = 16
PIECE = LAYERS * OWN
TOTALS = 2 * SIDE // LAYERS
HALF = PEERS // 2
BF16, F32 = jnp.bfloat16, jnp.float32
VMEM = pl.BlockSpec(memory_space=pltpu.VMEM)
SMEM = pl.BlockSpec(memory_space=pltpu.SMEM)
PARAMS = pltpu.CompilerParams(vmem_limit_bytes=24 << 20)


def cost(rows, n):
    return pl.CostEstimate(flops=2 * rows * n * WIDTH, bytes_accessed=1 << 20, transcendentals=0)


def sum_body(cell_ref, measures_ref, totals_ref):
    cell = cell_ref[...]
    label = lax.broadcasted_iota(jnp.int32, (SIDE, cell.shape[1]), 0)
    in_region = (label == (cell >> 6)).astype(F32).astype(BF16)
    in_product = (label == (cell & 63)).astype(F32).astype(BF16)
    member = jnp.concatenate([in_region, in_product], axis=0)
    totals = jnp.dot(member, measures_ref[...], preferred_element_type=F32)
    totals_ref[...] = totals.reshape(LAYERS, TOTALS, WIDTH)


def sum_labels(cell, measures):
    return pl.pallas_call(
        sum_body,
        out_shape=jax.ShapeDtypeStruct((LAYERS, TOTALS, WIDTH), F32),
        in_specs=[VMEM, VMEM],
        out_specs=VMEM,
        compiler_params=PARAMS,
        cost_estimate=cost(128, cell.shape[1]),
        name="sum_labels",
    )(cell, measures)


def prep_body(core_ref, cell_ref, table_ref, code_ref):
    slot = table_ref[...]
    far = ((slot >> 5) & 1) ^ core_ref[0]
    plane = ((slot >> 6) & 7) * 2 + ((slot >> 4) & 1)
    high = far * 32 + plane * 2 + (slot >> 11)
    low = ((slot >> 9) & 3) * 16 + (slot & 15)
    both = jnp.concatenate([high * 64, low], axis=0).astype(F32).astype(BF16)
    cell = cell_ref[...]
    label = lax.broadcasted_iota(jnp.int32, (SIDE, cell.shape[1]), 0)
    in_line = ((label & 31) == (cell >> 7)).astype(F32).astype(BF16)
    found = lax.dot_general(both, in_line, (((0,), (0,)), ((), ())), preferred_element_type=F32)
    place = lax.broadcasted_iota(jnp.int32, found.shape, 0) == (cell & 127)
    code_ref[...] = jnp.sum(jnp.where(place, found, 0.0), axis=0, keepdims=True).astype(jnp.int32)


def prep(core, cell, table):
    return pl.pallas_call(
        prep_body,
        out_shape=jax.ShapeDtypeStruct(cell.shape, jnp.int32),
        in_specs=[SMEM, VMEM, VMEM],
        out_specs=VMEM,
        compiler_params=PARAMS,
        cost_estimate=cost(256, cell.shape[1]),
        name="prep",
    )(core, cell, table)


def half_sums(first, code_ref, measures_ref, line_ref, lhs_ref):
    group = code_ref[...] >> 6
    for k in range(2 * HALF):
        chosen = (group == first + k).astype(F32).astype(BF16)
        lhs_ref[k * SIDE : (k + 1) * SIDE, :] = line_ref[...] * chosen
    return jnp.dot(lhs_ref[...], measures_ref[...], preferred_element_type=F32)


def set_lines(code_ref, line_ref):
    label = lax.broadcasted_iota(jnp.int32, line_ref.shape, 0)
    line_ref[...] = (label == (code_ref[...] & 63)).astype(F32).astype(BF16)


def send_body(first, code_ref, measures_ref, out_ref, line_ref, lhs_ref):
    set_lines(code_ref, line_ref)
    sums = half_sums(first, code_ref, measures_ref, line_ref, lhs_ref)
    out_ref[...] = sums.reshape(HALF, PIECE, WIDTH)


def scratch(n):
    return [pltpu.VMEM((SIDE, n), BF16), pltpu.VMEM((HALF * PIECE, n), BF16)]


def send(first, code, measures):
    n = code.shape[1]
    return pl.pallas_call(
        functools.partial(send_body, first),
        out_shape=jax.ShapeDtypeStruct((HALF, PIECE, WIDTH), F32),
        in_specs=[VMEM, VMEM],
        out_specs=VMEM,
        scratch_shapes=scratch(n),
        compiler_params=PARAMS,
        cost_estimate=cost(HALF * PIECE, n),
        name="send",
    )(code, measures)


def keep_body(code_ref, measures_ref, got0_ref, got1_ref, totals_ref, out_ref, line_ref, lhs_ref):
    set_lines(code_ref, line_ref)
    for half, got_ref in enumerate((got0_ref, got1_ref)):
        sums = half_sums(half * 2 * HALF, code_ref, measures_ref, line_ref, lhs_ref)
        out_ref[half * HALF : (half + 1) * HALF, 0:PIECE, :] = (
            sums.reshape(HALF, PIECE, WIDTH) + got_ref[...]
        )
    totals = jnp.sum(totals_ref[...], axis=0)
    for peer in range(PEERS):
        out_ref[peer, PIECE:, :] = totals


def keep(code, measures, got0, got1, totals):
    n = code.shape[1]
    return pl.pallas_call(
        keep_body,
        out_shape=jax.ShapeDtypeStruct((PEERS, PIECE + TOTALS, WIDTH), F32),
        in_specs=[VMEM] * 5,
        out_specs=VMEM,
        scratch_shapes=scratch(n),
        compiler_params=PARAMS,
        cost_estimate=cost(PEERS * PIECE, n),
        name="keep",
    )(code, measures, got0, got1, totals)


def column_body(near_ref, out_ref):
    out_ref[:, 0:OWN, :] = jnp.sum(near_ref[:, 0:PIECE, :], axis=0).reshape(LAYERS, OWN, WIDTH)
    totals = jnp.sum(near_ref[:, PIECE:, :], axis=0)
    for layer in range(LAYERS):
        out_ref[layer, OWN:, :] = totals


def column(near):
    return pl.pallas_call(
        column_body,
        out_shape=jax.ShapeDtypeStruct((LAYERS, OWN + TOTALS, WIDTH), F32),
        in_specs=[VMEM],
        out_specs=VMEM,
        compiler_params=PARAMS,
        name="column",
    )(near)


def last_body(far_ref, cube_ref, totals_ref):
    totals_ref[...] = far_ref[:, OWN:, :].reshape(2 * SIDE, WIDTH)
    cube_ref[...] = jnp.sum(far_ref[:, 0:OWN, :], axis=0)


def last(far):
    return pl.pallas_call(
        last_body,
        out_shape=[
            jax.ShapeDtypeStruct((OWN, WIDTH), F32),
            jax.ShapeDtypeStruct((2 * SIDE, WIDTH), F32),
        ],
        in_specs=[VMEM],
        out_specs=[VMEM, VMEM],
        compiler_params=PARAMS,
        name="last",
    )(far)


def both_body(mine_ref, other_ref, region_ref, product_ref):
    region_ref[...] = mine_ref[0:SIDE, :] + other_ref[0:SIDE, :]
    product_ref[...] = mine_ref[SIDE:, :] + other_ref[SIDE:, :]


def both(mine, other):
    total = jax.ShapeDtypeStruct((SIDE, WIDTH), F32)
    return pl.pallas_call(
        both_body,
        out_shape=[total, total],
        in_specs=[VMEM, VMEM],
        out_specs=[VMEM, VMEM],
        compiler_params=PARAMS,
        name="both",
    )(mine, other)


def to_partner(array):
    return lax.ppermute(array, CORE, [(0, 1), (1, 0)])


def exchange(array, axes):
    return lax.all_to_all(array, axes, 0, 0, tiled=True)


def on_device(region_id, product_id, measures, slot_of_cell):
    core = lax.axis_index(CORE)
    table = slot_of_cell.reshape(32, 128)
    cell = (region_id * SIDE + product_id)[None, :]
    totals = sum_labels(cell, measures)
    layer_totals = exchange(totals, Z)
    code = prep(core[None], cell, table)
    sent0 = send(32, code, measures)
    got0 = to_partner(sent0)
    code, sent0 = lax.optimization_barrier((code, sent0))
    sent1 = send(48, code, measures)
    got1 = to_partner(sent1)
    chip = keep(code, measures, got0, got1, layer_totals)
    far = exchange(column(exchange(chip, PLANE)), Z)
    cube, mine = last(far)
    region_totals, product_totals = both(mine, to_partner(mine))
    return cube, region_totals, product_totals


def solution(mesh):
    split = Mesh(mesh.devices.reshape(8, 4, 2, 2, mesh.shape["grp"]), ALL)
    in_specs = (P(ALL), P(ALL), P(ALL, None), P())
    out_specs = (P(ALL, None), P(), P())
    return jax.shard_map(
        on_device, mesh=split, in_specs=in_specs, out_specs=out_specs, check_vma=False
    )
```

time: 353 us -> 86.2 us (0.24)
  waiting for transfers between devices: 243 us -> 0.99 us
  blocking collectives: 18.8 us -> 61.6 us
  local copies, waits for them, and re-layouts: 33.3 us -> 2.3 us
  matrix products: 19 us -> 0 us
  between operations: 14.1 us -> 0.69 us
  other arithmetic: 12.5 us -> 0.74 us
  Pallas kernels: 0 us -> 11.7 us
  starting transfers between devices: 11.4 us -> 7.8 us
    psum x1 -> x0, waiting for transfers between devices: 197 us -> none  [on_device(): lax.psum((region_portion, product_part), ROWS_GRP)]
    all_to_all x1 -> x0, waiting for transfers between devices: 46.5 us -> none  [sum_in_two_steps(): lax.all_to_all(nearer, far, split_axis=0, concat_axis=0, tiled=True)]
    all_to_all x2 -> x3, blocking collectives: 18.8 us -> 61.6 us  [exchange(): return lax.all_to_all(array, axes, 0, 0, tiled=True)]
    gather x1 -> x0, local copies, waits for them, and re-layouts: 23 us -> none  [on_device(): slot = jnp.take(slot_of_cell, cell)]
    dot_general x10 -> x0, matrix products: 19 us -> none  [the longest x8 16.9 us: one_block(): return jnp.dot(onehot, measures, preferred_element_type=jnp.float32)]
    pallas_call x0 -> x8, Pallas kernels: none -> 11.7 us  [the longest x2 4.66 us: send(): pl.pallas_call(functools.partial(send_body, first), out_shape=jax.ShapeDt...]
    all_to_all x1 -> x0, starting transfers between devices: 11.3 us -> none  [sum_in_two_steps(): lax.all_to_all(nearer, far, split_axis=0, concat_axis=0, tiled=True)]
    ppermute x0 -> x3, starting transfers between devices: none -> 7.8 us  [to_partner(): return lax.ppermute(array, CORE, [(0, 1), (1, 0)])]
  transfers between devices with their start and end apart: 2 -> 3, of which waited for: 2 -> 1; matrix products, arithmetic and copies ran while one was open for 1% -> 0% of each run, Pallas kernels for 0% -> 1%
where the time goes in v2:
time: 86.2 us; the launch traced here: 85.8 us
  blocking collectives  61.6 us (71%)
  Pallas kernels  11.7 us (14%)
  starting transfers between devices  7.8 us (9%)
  local copies, waits for them, and re-layouts  2.3 us (3%)
  waiting for transfers between devices  0.99 us (1%)
    all_to_all x3, blocking collectives, exchange(): return lax.all_to_all(array, axes, 0, 0, tiled=True)  61.6 us
    ppermute x3, starting transfers between devices, to_partner(): return lax.ppermute(array, CORE, [(0, 1), (1, 0)])  7.8 us
    pallas_call x2, Pallas kernels, send(): pl.pallas_call(functools.partial(send_body, first), out_shape=jax.ShapeDt...  4.66 us
    pallas_call x1, Pallas kernels, keep(): pl.pallas_call(keep_body, out_shape=jax.ShapeDtypeStruct((PEERS, PIECE +...  4.63 us
    unnamed x4, local copies, waits for them, and re-layouts  2.3 us
  transfers between devices with their start and end apart: 3, of which 1 were waited for; matrix products, arithmetic and copies ran while one was open for 0% of the time, Pallas kernels for 1%

profile of v2, /device:TPU:1, one launch (start us, length us, event | category | flops | bytes accessed | tf_op | source)
XLA Modules:
  0.0 85.8 jit_solution(18443737936077125078)
XLA Ops:
  0.6 0.7 multiply_add_fusion
  1.4 0.0 copy-start.1
  1.4 0.7 copy-done.1
  2.1 0.5 prep.1.code_ref
  2.6 0.0 copy-start
  2.7 1.6 %copy-done = bf16[4096,256]{1,0:T(8,128)(2,1)S(1)} copy-done((bf16[4096,256]{1,0:T(8,128)(2,1)S(1)}, bf16[4096,256]{1,0:T(8,128)(2,1)}, u32[]{:S(2)}) %copy-start) | copy-done | bytes 2097176
  4.2 2.3 %send.2 = f32[8,128,256]{2,1,0:T(8,128)S(1)} custom-call(s32[1,4096]{1,0:T(1,128)S(1)} %prep.1.code_ref, bf16[4096,256]{1,0:T(8,128)(2,1)S(1)} %copy-done), custom_call_target="tpu_custom_call" | custom-call | flops 2147483648 | bytes 1048576 | tf_op jit(solution)/shard_map/send/pallas_call | solution.py:107
  6.6 2.3 %send.3 = f32[8,128,256]{2,1,0:T(8,128)S(1)} custom-call(s32[1,4096]{1,0:T(1,128)S(1)} %prep.1.code_ref, bf16[4096,256]{1,0:T(8,128)(2,1)S(1)} %copy-done), custom_call_target="tpu_custom_call" | custom-call | flops 2147483648 | bytes 1048576 | tf_op jit(solution)/shard_map/send/pallas_call | solution.py:107
  8.9 3.3 %collective-permute-start.1 = (f32[8,128,256]{2,1,0:T(8,128)S(1)}, f32[8,128,256]{2,1,0:T(8,128)S(1)}, u32[]{:S(2)}, u32[]{:S(2)}) collective-permute-start(f32[8,128,256]{2,1,0:T(8,128)S(1)} %send.3), channel_id=1, source_target_pairs={{0,2},{2,0},{1,3},{3,1},{4,6},{6,4},{5,7},{7,5},{8,10},{10,8},{9,1... | collective-permute-start | bytes 3145736 | tf_op jit(solution)/shard_map/ppermute | solution.py:200
  12.2 0.1 collective-permute-start
  12.3 0.4 sum_labels.1
  12.8 14.1 %all_to_all.15.totals_ref = f32[8,16,256]{2,1,0:T(8,128)S(1)} all-to-all(f32[8,16,256]{2,1,0:T(8,128)S(1)} %sum_labels.1), channel_id=1, replica_groups=mesh['rows_0'=8,'rows_1'=4,'rows_2'=2,'rows_3'=2,'grp'=2] {'rows_0'}, dimensions={0} | all-to-all | bytes 262144 | tf_op jit(solution)/shard_map/all_to_all | solution.py:204
  26.9 0.0 collective-permute-done.1.got1_ref
  26.9 0.0 collective-permute-done.got0_ref
  26.9 4.6 %keep.1 = f32[16,144,256]{2,1,0:T(8,128)S(1)} custom-call(s32[1,4096]{1,0:T(1,128)S(1)} %prep.1.code_ref, bf16[4096,256]{1,0:T(8,128)(2,1)S(1)} %copy-done, f32[8,128,256]{2,1,0:T(8,128)S(1)} %collective-permute-done.got0_ref, f32[8,128,256]{2,1,0:T(8,128)S(1)} %collective-permute-done.1.got1_ref, f32[8,16,256]{2,1,0:T(8,128)S(1)} %all_to_all.15.totals_ref), custom_call_target="tpu_custom_call" | custom-call | flops 4294967296 | bytes 1048576 | tf_op jit(solution)/shard_map/keep/pallas_call | solution.py:133
  31.5 34.9 %all_to_all.16.near_ref = f32[16,144,256]{2,1,0:T(8,128)S(1)} all-to-all(f32[16,144,256]{2,1,0:T(8,128)S(1)} %keep.1), channel_id=1, replica_groups=mesh['rows_0'=8,'rows_1'=4,'rows_2'=2,'rows_3'=2,'grp'=2] {'rows_1','row..., dimensions={0} | all-to-all | bytes 4718592 | tf_op jit(solution)/shard_map/all_to_all | solution.py:204
  66.4 0.1 column.1
  66.5 12.6 %all_to_all.17.far_ref = f32[8,32,256]{2,1,0:T(8,128)S(1)} all-to-all(f32[8,32,256]{2,1,0:T(8,128)S(1)} %column.1), channel_id=1, replica_groups=mesh['rows_0'=8,'rows_1'=4,'rows_2'=2,'rows_3'=2,'grp'=2] {'rows_0'}, dimensions={0} | all-to-all | bytes 524288 | tf_op jit(solution)/shard_map/all_to_all | solution.py:204
  79.1 0.6 last.1
  79.7 4.4 %collective-permute-start.2 = (f32[128,256]{1,0:T(8,128)S(1)}, f32[128,256]{1,0:T(8,128)S(1)}, u32[]{:S(2)}, u32[]{:S(2)}) collective-permute-start(f32[128,256]{1,0:T(8,128)S(1)} %get-tuple-element.10.mine_ref), channel_id=1, source_target_pairs={{0,2},{2,0},{1,3},{3,1},{4,6},{6,4},{5,7},{7,5},{8,10},{10,8},{9,1... | collective-permute-start | bytes 393224 | tf_op jit(solution)/shard_map/ppermute | solution.py:200
  84.1 1.0 %collective-permute-done.2.other_ref = f32[128,256]{1,0:T(8,128)S(1)} collective-permute-done((f32[128,256]{1,0:T(8,128)S(1)}, f32[128,256]{1,0:T(8,128)S(1)}, u32[]{:S(2)}, u32[]{:S(2)}) %collective-permute-start.2) | collective-permute-done | bytes 131104 | tf_op jit(solution)/shard_map/ppermute | solution.py:200
  85.1 0.7 both.1
Async XLA Ops:
  1.4 0.7 copy-start.1
  2.6 1.6 %copy-start = (bf16[4096,256]{1,0:T(8,128)(2,1)S(1)}, bf16[4096,256]{1,0:T(8,128)(2,1)}, u32[]{:S(2)}) copy-start(bf16[4096,256]{1,0:T(8,128)(2,1)} %measures_ref.7) | copy-start | bytes 6291460
  8.9 17.9 %collective-permute-start.1 = (f32[8,128,256]{2,1,0:T(8,128)S(1)}, f32[8,128,256]{2,1,0:T(8,128)S(1)}, u32[]{:S(2)}, u32[]{:S(2)}) collective-permute-start(f32[8,128,256]{2,1,0:T(8,128)S(1)} %send.3), channel_id=1, source_target_pairs={{0,2},{2,0},{1,3},{3,1},{4,6},{6,4},{5,7},{7,5},{8,10},{10,8},{9,1... | collective-permute-start | bytes 3145736 | tf_op jit(solution)/shard_map/ppermute | solution.py:200
  12.2 14.7 %collective-permute-start = (f32[8,128,256]{2,1,0:T(8,128)S(1)}, f32[8,128,256]{2,1,0:T(8,128)S(1)}, u32[]{:S(2)}, u32[]{:S(2)}) collective-permute-start(f32[8,128,256]{2,1,0:T(8,128)S(1)} %send.2), channel_id=1, source_target_pairs={{0,2},{2,0},{1,3},{3,1},{4,6},{6,4},{5,7},{7,5},{8,10},{10,8},{9,1... | collective-permute-start | bytes 3145736 | tf_op jit(solution)/shard_map/ppermute | solution.py:200
  79.7 5.4 %collective-permute-start.2 = (f32[128,256]{1,0:T(8,128)S(1)}, f32[128,256]{1,0:T(8,128)S(1)}, u32[]{:S(2)}, u32[]{:S(2)}) collective-permute-start(f32[128,256]{1,0:T(8,128)S(1)} %get-tuple-element.10.mine_ref), channel_id=1, source_target_pairs={{0,2},{2,0},{1,3},{3,1},{4,6},{6,4},{5,7},{7,5},{8,10},{10,8},{9,1... | collective-permute-start | bytes 393224 | tf_op jit(solution)/shard_map/ppermute | solution.py:200

commit v3 on v2

v3 whole, which is shorter than its diff:
```python
import functools

import jax
import jax.numpy as jnp
from jax import lax
from jax.experimental import pallas as pl
from jax.experimental.pallas import tpu as pltpu
from jax.sharding import Mesh
from jax.sharding import PartitionSpec as P


ALL = "all"
WIDTH = 256
SIDE = 64
OWN = 16
PEERS = 8
LATER = 16
PIECE = LATER * OWN
TOTALS = 2 * SIDE // LATER
HALF = PEERS // 2
PER_DOT = HALF * PIECE // SIDE
BF16, F32 = jnp.bfloat16, jnp.float32
VMEM = pl.BlockSpec(memory_space=pltpu.VMEM)
SMEM = pl.BlockSpec(memory_space=pltpu.SMEM)
PARAMS = pltpu.CompilerParams(vmem_limit_bytes=20 << 20)


def device(z, y, x, core):
    return (((z % 8 * 4 + y) * 2 + x % 2) * 2 + core) * 2 + x // 2


def member(core, a, pair, b, rest):
    return device(rest * 2 + pair + core, *((b, a) if core else (a, b)), core)


CHOICES = [(core, i, j) for core in range(2) for i in range(4) for j in range(4)]
FIRST = [
    [member(core, a, pair, b, rest) for a in range(4) for pair in range(2)]
    for core, b, rest in CHOICES
]
SECOND = [
    [member(core, a, pair, b, rest) for b in range(4) for rest in range(4)]
    for core, a, pair in [(c, i, j) for c in range(2) for i in range(4) for j in range(2)]
]
PARTNERS = [(d, d ^ 2) for d in range(256)]


def cost(rows, n):
    return pl.CostEstimate(flops=2 * rows * n * WIDTH, bytes_accessed=1 << 20, transcendentals=0)


def sum_body(cell_ref, measures_ref, totals_ref):
    cell = cell_ref[...]
    label = lax.broadcasted_iota(jnp.int32, (SIDE, cell.shape[1]), 0)
    in_region = (label == (cell >> 6)).astype(F32).astype(BF16)
    in_product = (label == (cell & 63)).astype(F32).astype(BF16)
    member = jnp.concatenate([in_region, in_product], axis=0)
    totals = jnp.dot(member, measures_ref[...], preferred_element_type=F32)
    totals_ref[...] = totals.reshape(LATER, TOTALS, WIDTH)


def sum_labels(cell, measures):
    return pl.pallas_call(
        sum_body,
        out_shape=jax.ShapeDtypeStruct((LATER, TOTALS, WIDTH), F32),
        in_specs=[VMEM, VMEM],
        out_specs=VMEM,
        compiler_params=PARAMS,
        cost_estimate=cost(128, cell.shape[1]),
        name="sum_labels",
    )(cell, measures)


def prep_body(core_ref, cell_ref, table_ref, code_ref):
    slot = table_ref[...]
    core = (slot >> 5) & 1
    y = (slot >> 7) & 3
    x = ((slot >> 4) & 1) * 2 + ((slot >> 6) & 1)
    z = ((slot >> 9) - core) & 7
    a, b = jnp.where(core == 0, y, x), jnp.where(core == 0, x, y)
    high = (core ^ core_ref[0]) * 32 + a * 8 + (z & 1) * 4 + b
    low = (z >> 1) * 16 + (slot & 15)
    both = jnp.concatenate([high * 64, low], axis=0).astype(F32).astype(BF16)
    cell = cell_ref[...]
    label = lax.broadcasted_iota(jnp.int32, (SIDE, cell.shape[1]), 0)
    in_line = ((label & 31) == (cell >> 7)).astype(F32).astype(BF16)
    found = lax.dot_general(both, in_line, (((0,), (0,)), ((), ())), preferred_element_type=F32)
    place = lax.broadcasted_iota(jnp.int32, found.shape, 0) == (cell & 127)
    code_ref[...] = jnp.sum(jnp.where(place, found, 0.0), axis=0, keepdims=True).astype(jnp.int32)


def prep(core, cell, table):
    return pl.pallas_call(
        prep_body,
        out_shape=jax.ShapeDtypeStruct(cell.shape, jnp.int32),
        in_specs=[SMEM, VMEM, VMEM],
        out_specs=VMEM,
        compiler_params=PARAMS,
        cost_estimate=cost(256, cell.shape[1]),
        name="prep",
    )(core, cell, table)


def half_sums(first, code_ref, measures_ref, line_ref, lhs_ref):
    group = code_ref[...] >> 6
    for k in range(PER_DOT):
        chosen = (group == first + k).astype(F32).astype(BF16)
        lhs_ref[k * SIDE : (k + 1) * SIDE, :] = line_ref[...] * chosen
    return jnp.dot(lhs_ref[...], measures_ref[...], preferred_element_type=F32)


def set_lines(code_ref, line_ref):
    label = lax.broadcasted_iota(jnp.int32, line_ref.shape, 0)
    line_ref[...] = (label == (code_ref[...] & 63)).astype(F32).astype(BF16)


def block_body(first, code_ref, measures_ref, out_ref, line_ref, lhs_ref):
    set_lines(code_ref, line_ref)
    for half in range(2):
        sums = half_sums(first + half * PER_DOT, code_ref, measures_ref, line_ref, lhs_ref)
        out_ref[half * HALF : (half + 1) * HALF] = sums.reshape(HALF, PIECE, WIDTH)


def block(first, code, measures):
    n = code.shape[1]
    return pl.pallas_call(
        functools.partial(block_body, first),
        out_shape=jax.ShapeDtypeStruct((PEERS, PIECE, WIDTH), F32),
        in_specs=[VMEM, VMEM],
        out_specs=VMEM,
        scratch_shapes=[pltpu.VMEM((SIDE, n), BF16), pltpu.VMEM((HALF * PIECE, n), BF16)],
        compiler_params=PARAMS,
        cost_estimate=cost(PEERS * PIECE, n),
        name="block",
    )(code, measures)


def join_body(mine_ref, got_ref, totals_ref, out_ref):
    out_ref[:, 0:PIECE, :] = mine_ref[...] + got_ref[...]
    totals = jnp.sum(totals_ref[...], axis=0)
    for peer in range(PEERS):
        out_ref[peer, PIECE:, :] = totals


def join(mine, got, totals):
    return pl.pallas_call(
        join_body,
        out_shape=jax.ShapeDtypeStruct((PEERS, PIECE + TOTALS, WIDTH), F32),
        in_specs=[VMEM] * 3,
        out_specs=VMEM,
        compiler_params=PARAMS,
        name="join",
    )(mine, got, totals)


def column_body(near_ref, out_ref):
    out_ref[:, 0:OWN, :] = jnp.sum(near_ref[:, 0:PIECE, :], axis=0).reshape(LATER, OWN, WIDTH)
    totals = jnp.sum(near_ref[:, PIECE:, :], axis=0)
    for layer in range(LATER):
        out_ref[layer, OWN:, :] = totals


def column(near):
    return pl.pallas_call(
        column_body,
        out_shape=jax.ShapeDtypeStruct((LATER, OWN + TOTALS, WIDTH), F32),
        in_specs=[VMEM],
        out_specs=VMEM,
        compiler_params=PARAMS,
        name="column",
    )(near)


def last_body(far_ref, cube_ref, totals_ref):
    totals_ref[...] = far_ref[:, OWN:, :].reshape(2 * SIDE, WIDTH)
    cube_ref[...] = jnp.sum(far_ref[:, 0:OWN, :], axis=0)


def last(far):
    return pl.pallas_call(
        last_body,
        out_shape=[
            jax.ShapeDtypeStruct((OWN, WIDTH), F32),
            jax.ShapeDtypeStruct((2 * SIDE, WIDTH), F32),
        ],
        in_specs=[VMEM],
        out_specs=[VMEM, VMEM],
        compiler_params=PARAMS,
        name="last",
    )(far)


def both_body(mine_ref, other_ref, region_ref, product_ref):
    region_ref[...] = mine_ref[0:SIDE, :] + other_ref[0:SIDE, :]
    product_ref[...] = mine_ref[SIDE:, :] + other_ref[SIDE:, :]


def both(mine, other):
    total = jax.ShapeDtypeStruct((SIDE, WIDTH), F32)
    return pl.pallas_call(
        both_body,
        out_shape=[total, total],
        in_specs=[VMEM, VMEM],
        out_specs=[VMEM, VMEM],
        compiler_params=PARAMS,
        name="both",
    )(mine, other)


def to_partner(array):
    return lax.ppermute(array, ALL, PARTNERS)


def exchange(array, groups):
    return lax.all_to_all(array, ALL, 0, 0, axis_index_groups=groups, tiled=True)


def on_device(region_id, product_id, measures, slot_of_cell):
    core = (lax.axis_index(ALL) >> 1) & 1
    table = slot_of_cell.reshape(32, 128)
    cell = (region_id * SIDE + product_id)[None, :]
    totals = sum_labels(cell, measures)
    some_totals = exchange(totals, SECOND)
    code = prep(core[None], cell, table)
    sent = block(32, code, measures)
    got = to_partner(sent)
    code, sent, some_totals = lax.optimization_barrier((code, sent, some_totals))
    mine = block(0, code, measures)
    chip = join(mine, got, some_totals)
    far = exchange(column(exchange(chip, FIRST)), SECOND)
    cube, mine = last(far)
    region_totals, product_totals = both(mine, to_partner(mine))
    return cube, region_totals, product_totals


def solution(mesh):
    split = Mesh(mesh.devices.reshape(-1), (ALL,))
    in_specs = (P(ALL), P(ALL), P(ALL, None), P(None))
    out_specs = (P(ALL, None), P(), P())
    return jax.shard_map(
        on_device, mesh=split, in_specs=in_specs, out_specs=out_specs, check_vma=False
    )
```

time: 86.2 us -> 80.3 us (0.932); the launches traced: 85.8 us -> 78.9 us
  starting transfers between devices: 7.8 us -> 3.69 us
  blocking collectives: 61.6 us -> 58.7 us
    ppermute x3 -> x2, starting transfers between devices: 7.8 us -> 3.69 us  [to_partner(): return lax.ppermute(array, ALL, PARTNERS)]
    all_to_all x3, blocking collectives: 61.6 us -> 58.7 us  [exchange(): lax.all_to_all(array, ALL, 0, 0, axis_index_groups=groups, tiled=True)]
  transfers between devices with their start and end apart: 3 -> 2, of which waited for: 1 -> 1; matrix products, arithmetic and copies ran while one was open for 0% -> 0% of each run, Pallas kernels for 1% -> 6%
where the time goes in v3:
time: 80.3 us; the launch traced here: 78.9 us
  blocking collectives  58.7 us (73%)
  Pallas kernels  11.9 us (15%)
  starting transfers between devices  3.69 us (5%)
  local copies, waits for them, and re-layouts  2.3 us (3%)
  waiting for transfers between devices  0.99 us (1%)
    all_to_all x3, blocking collectives, exchange(): lax.all_to_all(array, ALL, 0, 0, axis_index_groups=groups, tiled=True)  58.7 us
    pallas_call x2, Pallas kernels, block(): pl.pallas_call(functools.partial(block_body, first), out_shape=jax.ShapeD...  9.25 us
    ppermute x2, starting transfers between devices, to_partner(): return lax.ppermute(array, ALL, PARTNERS)  3.69 us
    unnamed x4, local copies, waits for them, and re-layouts  2.3 us
  transfers between devices with their start and end apart: 2, of which 1 were waited for; matrix products, arithmetic and copies ran while one was open for 0% of the time, Pallas kernels for 6%

profile of v3, /device:TPU:1, one launch (start us, length us, event | category | flops | bytes accessed | tf_op | source)
XLA Modules:
  0.0 78.9 jit_solution(14325366816176214204)
XLA Ops:
  0.6 0.7 multiply_add_fusion
  1.4 0.0 copy-start.1
  1.4 0.7 copy-done.1
  2.1 0.5 prep.1.code_ref
  2.6 0.0 copy-start
  2.7 1.6 %copy-done = bf16[4096,256]{1,0:T(8,128)(2,1)S(1)} copy-done((bf16[4096,256]{1,0:T(8,128)(2,1)S(1)}, bf16[4096,256]{1,0:T(8,128)(2,1)}, u32[]{:S(2)}) %copy-start) | copy-done | bytes 2097176
  4.2 4.6 %block.2 = f32[8,256,256]{2,1,0:T(8,128)S(1)} custom-call(s32[1,4096]{1,0:T(1,128)S(1)} %prep.1.code_ref, bf16[4096,256]{1,0:T(8,128)(2,1)S(1)} %copy-done), custom_call_target="tpu_custom_call" | custom-call | flops 4294967296 | bytes 1048576 | tf_op jit(solution)/shard_map/block/pallas_call | solution.py:126
  8.9 3.3 %collective-permute-start = (f32[8,256,256]{2,1,0:T(8,128)S(1)}, f32[8,256,256]{2,1,0:T(8,128)S(1)}, u32[]{:S(2)}, u32[]{:S(2)}) collective-permute-start(f32[8,256,256]{2,1,0:T(8,128)S(1)} %block.2), channel_id=1, source_target_pairs={{0,2},{1,3},{2,0},{3,1},{4,6},{5,7},{6,4},{7,5},{8,10},{9,11},{10,... | collective-permute-start | bytes 6291464 | tf_op jit(solution)/shard_map/ppermute | solution.py:211
  12.2 0.4 sum_labels.1
  12.6 19.5 %all_to_all.15.totals_ref = f32[16,8,256]{2,1,0:T(8,128)S(1)} all-to-all(f32[16,8,256]{2,1,0:T(8,128)S(1)} %sum_labels.1), channel_id=1, replica_groups={{0,64,128,192,4,68,132,196,1,65,129,193,5,69,133,197},{32,96,160,224,36..., dimensions={0} | all-to-all | bytes 262144 | tf_op jit(solution)/shard_map/all_to_all | solution.py:215
  32.1 4.6 %block.3.mine_ref = f32[8,256,256]{2,1,0:T(8,128)S(1)} custom-call(s32[1,4096]{1,0:T(1,128)S(1)} %prep.1.code_ref, bf16[4096,256]{1,0:T(8,128)(2,1)S(1)} %copy-done), custom_call_target="tpu_custom_call" | custom-call | flops 4294967296 | bytes 1048576 | tf_op jit(solution)/shard_map/block/pallas_call | solution.py:126
  36.7 0.0 collective-permute-done.got_ref
  36.8 0.2 join.1
  37.0 21.5 %all_to_all.16.near_ref = f32[8,264,256]{2,1,0:T(8,128)S(1)} all-to-all(f32[8,264,256]{2,1,0:T(8,128)S(1)} %join.1), channel_id=1, replica_groups={{0,32,8,40,16,48,24,56},{64,96,72,104,80,112,88,120},{128,160,136,168,1..., dimensions={0} | all-to-all | bytes 4325376 | tf_op jit(solution)/shard_map/all_to_all | solution.py:215
  58.5 0.1 column.1
  58.6 17.7 %all_to_all.17.far_ref = f32[16,24,256]{2,1,0:T(8,128)S(1)} all-to-all(f32[16,24,256]{2,1,0:T(8,128)S(1)} %column.1), channel_id=1, replica_groups={{0,64,128,192,4,68,132,196,1,65,129,193,5,69,133,197},{32,96,160,224,36..., dimensions={0} | all-to-all | bytes 786432 | tf_op jit(solution)/shard_map/all_to_all | solution.py:215
  76.3 0.6 last.1
  76.9 0.4 collective-permute-start.1
  77.3 1.0 %collective-permute-done.1.other_ref = f32[128,256]{1,0:T(8,128)S(1)} collective-permute-done((f32[128,256]{1,0:T(8,128)S(1)}, f32[128,256]{1,0:T(8,128)S(1)}, u32[]{:S(2)}, u32[]{:S(2)}) %collective-permute-start.1) | collective-permute-done | bytes 131104 | tf_op jit(solution)/shard_map/ppermute | solution.py:211
  78.3 0.7 both.1
Async XLA Ops:
  1.4 0.7 copy-start.1
  2.6 1.6 %copy-start = (bf16[4096,256]{1,0:T(8,128)(2,1)S(1)}, bf16[4096,256]{1,0:T(8,128)(2,1)}, u32[]{:S(2)}) copy-start(bf16[4096,256]{1,0:T(8,128)(2,1)} %measures_ref.5) | copy-start | bytes 6291460
  8.9 27.9 %collective-permute-start = (f32[8,256,256]{2,1,0:T(8,128)S(1)}, f32[8,256,256]{2,1,0:T(8,128)S(1)}, u32[]{:S(2)}, u32[]{:S(2)}) collective-permute-start(f32[8,256,256]{2,1,0:T(8,128)S(1)} %block.2), channel_id=1, source_target_pairs={{0,2},{1,3},{2,0},{3,1},{4,6},{5,7},{6,4},{7,5},{8,10},{9,11},{10,... | collective-permute-start | bytes 6291464 | tf_op jit(solution)/shard_map/ppermute | solution.py:211
  76.9 1.4 %collective-permute-start.1 = (f32[128,256]{1,0:T(8,128)S(1)}, f32[128,256]{1,0:T(8,128)S(1)}, u32[]{:S(2)}, u32[]{:S(2)}) collective-permute-start(f32[128,256]{1,0:T(8,128)S(1)} %get-tuple-element.12.mine_ref), channel_id=1, source_target_pairs={{0,2},{1,3},{2,0},{3,1},{4,6},{5,7},{6,4},{7,5},{8,10},{9,11},{10,... | collective-permute-start | bytes 393224 | tf_op jit(solution)/shard_map/ppermute | solution.py:211
